TPU v7x, 32 devices: a whole 2x2x4 slice. The times are simulated.
32 devices in a mesh: dp: 2 (over y), space: 16 (over z, x, core).
Axes of the slice: x: 2, y: 2, z: 4, core: 2. Of those that a mesh axis runs over, the one named last changes fastest.
Arguments:
- queries: bfloat16 [16, 200, 256], P('dp'), may hold values from -6 to 6
- query_pos: bfloat16 [200, 256], replicated, may hold values from -6 to 6
- pixels: bfloat16 [16, 4096, 256], P('dp', 'space'), may hold values from -160 to 160
- pixel_pos: bfloat16 [4096, 256], P('space'), may hold values from -6 to 6
- masks: int32 [16, 200, 4096], P('dp', None, 'space'), may hold values from 0 to 1, as said below
- wq_cross: bfloat16 [256, 256], replicated, may hold values from -0.375 to 0.375
- wk_cross: bfloat16 [256, 256], replicated, may hold values from -0.375 to 0.375
- wv_cross: bfloat16 [256, 256], replicated, may hold values from -0.375 to 0.375
- wo_cross: bfloat16 [256, 256], replicated, may hold values from -0.375 to 0.375
- gain_cross: float32 [256], replicated, may hold values from 0.1 to 1.9
- w_qkv: bfloat16 [256, 768], replicated, may hold values from -0.375 to 0.375
- wo_self: bfloat16 [256, 256], replicated, may hold values from -0.375 to 0.375
- gain_self: float32 [256], replicated, may hold values from 0.1 to 1.9
- w_in: bfloat16 [256, 2048], replicated, may hold values from -0.375 to 0.375
- w_out: bfloat16 [2048, 256], replicated, may hold values from -0.125 to 0.125
- gain_ffn: float32 [256], replicated, may hold values from 0.1 to 1.9
Outputs:
- new_queries: bfloat16 [16, 200, 256], P('dp')
Inputs may be any that keep to these rules, and one draw needn't show every extreme that they name: `masks`: 0 or 1; each row's ones lie within a run of at most 768 consecutive pixels, which may lie anywhere in the image; a row may have no ones on some devices' pixels or on all pixels of its image.
All inputs are finite; a program needn't handle non-finite values.
Results may differ from a plain program's by a relative error of at most 0.017.
The roundings to bfloat16 on the way count: a program that leaves them out, or rounds other values in their place, can miss the bound.
Values may be sent and summed in bfloat16 or wider, within the bound.
A program may use at most 128 MiB of HBM per device.

v0:
```python
import functools

import jax
import jax.numpy as jnp
from jax import lax
from jax.experimental import pallas as pl
from jax.experimental.pallas import tpu as pltpu
from jax.sharding import PartitionSpec as P

HEADS = 8
NEG = -1e30
MESH = pl.DeviceIdType.MESH
F32 = jnp.float32
BF16 = jnp.bfloat16


def nn(a, b):
    return lax.dot_general(a, b, (((1,), (0,)), ((), ())), preferred_element_type=F32)


def nt(a, b):
    return lax.dot_general(a, b, (((1,), (1,)), ((), ())), preferred_element_type=F32)


def eye(size):
    rows = lax.broadcasted_iota(jnp.int32, (size, size), 0)
    cols = lax.broadcasted_iota(jnp.int32, (size, size), 1)
    return jnp.where(rows == cols, 1.0, 0.0).astype(BF16)


def layer_norm(x, gain):
    mean = jnp.mean(x, axis=-1, keepdims=True)
    var = jnp.mean((x - mean) * (x - mean), axis=-1, keepdims=True)
    return (x - mean) / jnp.sqrt(var + 1e-05) * gain


def kernel(
    n,
    queries,
    query_pos,
    pixels,
    pixel_pos,
    masks,
    wq_cross,
    wk_cross,
    wv_cross,
    wo_cross,
    gain_cross,
    w_qkv,
    wo_self,
    gain_self,
    w_in,
    w_out,
    gain_ffn,
    out,
    q_mine,
    q_res,
    qpos_v,
    pix_v,
    pos_v,
    mask_v,
    wq_v,
    wk_v,
    wv_v,
    woc_v,
    gc_v,
    wqkv_v,
    wos_v,
    gs_v,
    win_v,
    wout_v,
    gf_v,
    wqt,
    wvt,
    wvst,
    send_s,
    send_t,
    recv_s,
    recv_t,
    att,
    gath,
    load_sem,
    pix_sem,
    mask_sem,
    xpix_s,
    xpix_r,
    xmask_s,
    xmask_r,
    xpos_s,
    xpos_r,
    ss_sem,
    st_sem,
    rs_sem,
    rt_sem,
    att_s,
    att_r,
    g1_s,
    g2_s,
    g_r,
    out_sem,
):
    images, nq, width = queries.shape
    npix = pixels.shape[1]
    half = images // 2
    npairs = n // 2
    spread = npairs // images
    hp = HEADS // 2
    hd = width // HEADS
    part = width // 2
    scale = 1.4426950408889634 / float(hd) ** 0.5

    me = lax.axis_index("space")
    core = lax.rem(me, 2)
    pair = lax.div(me, 2)
    other = 1 - core
    mate = pair * 2 + other
    base = core * half
    base_other = other * half
    my_image = lax.div(pair, spread)

    def remote(src, dst, ssem, rsem, dev):
        return pltpu.make_async_remote_copy(
            src_ref=src,
            dst_ref=dst,
            send_sem=ssem,
            recv_sem=rsem,
            device_id={"space": dev},
            device_id_type=MESH,
        )

    barrier = pltpu.get_barrier_semaphore()

    def greet(k, carry):
        dev = lax.rem(me + k, n)
        pl.semaphore_signal(barrier, inc=1, device_id={"space": dev}, device_id_type=MESH)
        return carry

    lax.fori_loop(1, n, greet, 0)

    loads = [
        (query_pos, qpos_v),
        (queries.at[pl.ds(base, half)], q_mine),
        (wq_cross, wq_v),
        (wk_cross, wk_v),
        (wv_cross, wv_v),
        (pixel_pos, pos_v.at[0]),
        (queries.at[my_image], q_res),
        (wo_cross, woc_v),
        (gain_cross, gc_v),
        (w_qkv, wqkv_v),
        (wo_self, wos_v),
        (gain_self, gs_v),
        (w_in, win_v),
        (w_out, wout_v),
        (gain_ffn, gf_v),
    ]
    load = [pltpu.make_async_copy(s, d, load_sem.at[i]) for i, (s, d) in enumerate(loads)]
    for c in load[:6]:
        c.start()
    pix_own = pltpu.make_async_copy(pixels.at[pl.ds(base, half)], pix_v.at[0], pix_sem)
    mask_own = pltpu.make_async_copy(masks.at[pl.ds(base, half)], mask_v.at[0], mask_sem)
    pix_own.start()
    mask_own.start()

    ident = eye(npix)
    for c in load[:6]:
        c.wait()
    wqt[...] = nt(eye(width), wq_v[...]).astype(BF16)
    wvt[...] = nt(eye(width), wv_v[...]).astype(BF16)

    pl.semaphore_wait(barrier, n - 1)
    xpos = remote(pixel_pos, pos_v.at[1], xpos_s, xpos_r, mate)
    xpos.start()

    def xpix(j):
        return remote(
            pixels.at[base_other + j], pix_v.at[1, j], xpix_s.at[j], xpix_r.at[j], mate
        )

    def xmask(j):
        return remote(
            masks.at[base_other + j], mask_v.at[1, j], xmask_s.at[j], xmask_r.at[j], mate
        )

    for j in range(half):
        xmask(j).start()
        xpix(j).start()
    for c in load[6:]:
        c.start()
    pix_own.wait()
    mask_own.wait()
    xpos.wait()

    def send_s_copy(j, o):
        owner = (base + j) * spread * 2 + o
        return owner, remote(
            send_s.at[j, o], recv_s.at[pair], ss_sem.at[j, o], rs_sem.at[pair], owner
        )

    def send_t_copy(j, o):
        owner = (base + j) * spread * 2 + o
        return owner, remote(
            send_t.at[j, o], recv_t.at[pair], st_sem.at[j, o], rt_sem.at[pair], owner
        )

    def one_image(j, carry):
        xmask(j).wait()
        xpix(j).wait()
        qin = (q_mine[j].astype(F32) + qpos_v[...].astype(F32)).astype(BF16)
        cqt = nt(wqt[...], qin).astype(BF16)
        keys, values, seen = [], [], []
        for side in range(2):
            pix = pix_v[side, j]
            key_in = (pix.astype(F32) + pos_v[side].astype(F32)).astype(BF16)
            keys.append(nn(key_in, wk_v[...]).astype(BF16))
            values.append(nt(wvt[...], pix).astype(BF16))
            seen.append(nt(ident, mask_v[side, j].astype(F32).astype(BF16)))
        key = jnp.concatenate(keys, axis=0)
        value = jnp.concatenate(values, axis=1)
        seen = jnp.concatenate(seen, axis=0)
        found = jnp.max(seen, axis=0, keepdims=True)
        bias = jnp.where(jnp.logical_or(seen > 0.5, found < 0.5), 0.0, NEG)
        for h in range(HEADS):
            pieces = [cqt[h * hd : (h + 1) * hd]]
            if h:
                pieces.insert(0, jnp.zeros((h * hd, nq), BF16))
            if h < HEADS - 1:
                pieces.append(jnp.zeros((width - (h + 1) * hd, nq), BF16))
            score = nn(key, jnp.concatenate(pieces, axis=0)) + bias
            top = jnp.max(score, axis=0, keepdims=True)
            weight = jnp.exp2((score - top) * scale)
            total = jnp.sum(weight, axis=0, keepdims=True)
            summed = nn(value[h * hd : (h + 1) * hd], weight.astype(BF16))
            o, r = h // hp, h % hp
            send_s[j, o, r * hd : (r + 1) * hd, :] = summed.astype(BF16)
            send_t[j, o, r : r + 1, :] = top
            send_t[j, o, hp + r : hp + r + 1, :] = total
        for o in range(2):
            send_t[j, o, 2 * hp : 2 * hp + 1, :] = found
        for o in range(2):
            owner, copy_s = send_s_copy(j, o)
            _, copy_t = send_t_copy(j, o)

            @pl.when(owner != me)
            def _():
                copy_t.start()
                copy_s.start()

            @pl.when(owner == me)
            def _():
                pltpu.make_async_copy(send_t.at[j, o], recv_t.at[pair], rt_sem.at[pair]).start()
                pltpu.make_async_copy(send_s.at[j, o], recv_s.at[pair], rs_sem.at[pair]).start()

        return carry

    lax.fori_loop(0, half, one_image, 0)

    for c in load[6:]:
        c.wait()
    wvst[...] = nt(eye(width), wqkv_v[:, 2 * width :]).astype(BF16)

    def fold(k, carry):
        top, total, flag, acc = carry
        slot = lax.rem(pair + k, npairs)
        pltpu.make_async_copy(recv_t.at[slot], recv_t.at[slot], rt_sem.at[slot]).wait()
        pltpu.make_async_copy(recv_s.at[slot], recv_s.at[slot], rs_sem.at[slot]).wait()
        new_top = recv_t[slot, 0:hp, :]
        new_total = recv_t[slot, hp : 2 * hp, :]
        new_flag = recv_t[slot, 2 * hp : 2 * hp + 1, :]
        new = recv_s[slot].astype(F32)
        best = jnp.maximum(flag, new_flag)
        a = jnp.where(flag == best, top, NEG)
        b = jnp.where(new_flag == best, new_top, NEG)
        top = jnp.maximum(a, b)
        ea = jnp.exp2((a - top) * scale)
        eb = jnp.exp2((b - top) * scale)
        total = total * ea + new_total * eb
        acc = jnp.concatenate(
            [
                acc[r * hd : (r + 1) * hd] * ea[r : r + 1] + new[r * hd : (r + 1) * hd] * eb[r : r + 1]
                for r in range(hp)
            ],
            axis=0,
        )
        return top, total, best, acc

    def gather_copy(ssem, image, c, dev):
        ref = gath.at[image, c]
        return remote(ref, ref, ssem, g_r.at[image, c], dev)

    def owner_work():
        start = (
            jnp.full((hp, nq), NEG, F32),
            jnp.zeros((hp, nq), F32),
            jnp.full((1, nq), -1.0, F32),
            jnp.zeros((part, nq), F32),
        )
        top, total, flag, acc = lax.fori_loop(0, npairs, fold, start)
        mine = jnp.concatenate(
            [acc[r * hd : (r + 1) * hd] / total[r : r + 1] for r in range(hp)], axis=0
        ).astype(BF16)
        att[core] = mine
        swap = remote(att.at[core], att.at[core], att_s, att_r.at[core], mate)
        swap.start()
        pltpu.make_async_copy(att.at[other], att.at[other], att_r.at[other]).wait()
        attended_t = jnp.concatenate([att[0], att[1]], axis=0)
        ident_q = eye(nq)
        attended = nt(ident_q, attended_t).astype(BF16)
        cross_proj = nn(attended, woc_v[...])
        after_cross = layer_norm(q_res[...].astype(F32) + cross_proj, gc_v[...]).astype(BF16)
        ac32 = after_cross.astype(F32)
        self_in = (ac32 + qpos_v[...].astype(F32)).astype(BF16)
        both = nn(self_in, wqkv_v[:, : 2 * width]).astype(BF16)
        sq, sk = both[:, :width], both[:, width:]
        svt = nt(wvst[...], after_cross).astype(BF16)
        lane_head = lax.broadcasted_iota(jnp.int32, (nq, width), 1) // hd
        outs = []
        for h in range(HEADS):
            key = jnp.where(lane_head == h, sk.astype(F32), 0.0).astype(BF16)
            logits = nt(key, sq)
            top = jnp.max(logits, axis=0, keepdims=True)
            expo = jnp.exp2((logits - top) * scale)
            weight = (expo / jnp.sum(expo, axis=0, keepdims=True)).astype(BF16)
            outs.append(nn(svt[h * hd : (h + 1) * hd], weight).astype(BF16))
        self_out = nt(ident_q, jnp.concatenate(outs, axis=0)).astype(BF16)
        self_proj = nn(self_out, wos_v[...])
        after_self = layer_norm(ac32 + self_proj, gs_v[...]).astype(BF16)
        hidden = jnp.maximum(nn(after_self, win_v[...]), 0.0).astype(BF16)
        ffn = nn(hidden, wout_v[...])
        result = layer_norm(after_self.astype(F32) + ffn, gf_v[...]).astype(BF16)
        for c in range(2):
            gath[my_image, c] = result[:, c * part : (c + 1) * part]

        def spread_out(k, carry):
            dev = lax.rem(pair + k, npairs) * 2 + core
            gather_copy(g1_s.at[k], my_image, core, dev).start()
            return carry

        lax.fori_loop(1, npairs, spread_out, 0)
        swap.wait_send()

    is_owner = lax.rem(pair, spread) == 0
    if spread == 1:
        owner_work()
    else:
        pl.when(is_owner)(owner_work)

    def write_out(image, c):
        return pltpu.make_async_copy(
            gath.at[image, c],
            out.at[image, :, pl.ds(pl.multiple_of(c * part, part), part)],
            out_sem.at[image, c],
        )

    def arrive_near(k, carry):
        image = lax.rem(my_image + k, images)
        not_mine = jnp.logical_or(image != my_image, jnp.logical_not(is_owner))

        @pl.when(not_mine)
        def _():
            ref = gath.at[image, core]
            pltpu.make_async_copy(ref, ref, g_r.at[image, core]).wait()
            gather_copy(g2_s.at[image], image, core, mate).start()

        write_out(image, core).start()
        return carry

    lax.fori_loop(0, images, arrive_near, 0)

    def arrive_far(k, carry):
        image = lax.rem(my_image + k, images)
        not_mine = jnp.logical_or(image != my_image, jnp.logical_not(is_owner))

        @pl.when(not_mine)
        def _():
            ref = gath.at[image, other]
            pltpu.make_async_copy(ref, ref, g_r.at[image, other]).wait()

        write_out(image, other).start()
        return carry

    lax.fori_loop(0, images, arrive_far, 0)

    def drain_sends(j, carry):
        for o in range(2):
            owner, copy_s = send_s_copy(j, o)
            _, copy_t = send_t_copy(j, o)

            @pl.when(owner != me)
            def _():
                copy_s.wait_send()
                copy_t.wait_send()

        return carry

    lax.fori_loop(0, half, drain_sends, 0)

    def drain_spread():
        def body(k, carry):
            dev = lax.rem(pair + k, npairs) * 2 + core
            gather_copy(g1_s.at[k], my_image, core, dev).wait_send()
            return carry

        lax.fori_loop(1, npairs, body, 0)

    if spread == 1:
        drain_spread()
    else:
        pl.when(is_owner)(drain_spread)

    def drain_out(image, carry):
        not_mine = jnp.logical_or(image != my_image, jnp.logical_not(is_owner))

        @pl.when(not_mine)
        def _():
            gather_copy(g2_s.at[image], image, core, mate).wait_send()

        for c in range(2):
            write_out(image, c).wait()
        return carry

    lax.fori_loop(0, images, drain_out, 0)


def local(n, *args):
    queries, query_pos, pixels, pixel_pos, masks = args[:5]
    args = list(args)
    for i in (9, 12, 15):
        args[i] = args[i].reshape(1, -1)
    images, nq, width = queries.shape
    npix = pixels.shape[1]
    half = images // 2
    npairs = n // 2
    part = width // 2
    hp = HEADS // 2
    ff = args[13].shape[1]
    dma = pltpu.SemaphoreType.DMA
    scratch = [
        pltpu.VMEM((half, nq, width), BF16),
        pltpu.VMEM((nq, width), BF16),
        pltpu.VMEM((nq, width), BF16),
        pltpu.VMEM((2, half, npix, width), BF16),
        pltpu.VMEM((2, npix, width), BF16),
        pltpu.VMEM((2, half, nq, npix), jnp.int32),
        pltpu.VMEM((width, width), BF16),
        pltpu.VMEM((width, width), BF16),
        pltpu.VMEM((width, width), BF16),
        pltpu.VMEM((width, width), BF16),
        pltpu.VMEM((1, width), F32),
        pltpu.VMEM((width, 3 * width), BF16),
        pltpu.VMEM((width, width), BF16),
        pltpu.VMEM((1, width), F32),
        pltpu.VMEM((width, ff), BF16),
        pltpu.VMEM((ff, width), BF16),
        pltpu.VMEM((1, width), F32),
        pltpu.VMEM((width, width), BF16),
        pltpu.VMEM((width, width), BF16),
        pltpu.VMEM((width, width), BF16),
        pltpu.VMEM((half, 2, part, nq), BF16),
        pltpu.VMEM((half, 2, 2 * hp + 1, nq), F32),
        pltpu.VMEM((npairs, part, nq), BF16),
        pltpu.VMEM((npairs, 2 * hp + 1, nq), F32),
        pltpu.VMEM((2, part, nq), BF16),
        pltpu.VMEM((images, 2, nq, part), BF16),
        dma((15,)),
        dma,
        dma,
        dma((half,)),
        dma((half,)),
        dma((half,)),
        dma((half,)),
        dma,
        dma,
        dma((half, 2)),
        dma((half, 2)),
        dma((npairs,)),
        dma((npairs,)),
        dma,
        dma((2,)),
        dma((npairs,)),
        dma((images,)),
        dma((images, 2)),
        dma((images, 2)),
    ]
    return pl.pallas_call(
        functools.partial(kernel, n),
        out_shape=jax.ShapeDtypeStruct((images, nq, width), BF16),
        in_specs=[pl.BlockSpec(memory_space=pl.ANY)] * len(args),
        out_specs=pl.BlockSpec(memory_space=pl.ANY),
        scratch_shapes=scratch,
        compiler_params=pltpu.CompilerParams(
            collective_id=0, has_side_effects=True, vmem_limit_bytes=60 * 1024 * 1024
        ),
    )(*args)


def solution(mesh):
    placed = (
        P("dp", None, None),
        P(),
        P("dp", "space", None),
        P("space", None),
        P("dp", None, "space"),
    ) + (P(),) * 11
    return jax.shard_map(
        functools.partial(local, mesh.shape["space"]),
        mesh=mesh,
        in_specs=placed,
        out_specs=P("dp", None, None),
        check_vma=False,
    )
```

profile of v0, /device:TPU:21, one launch (start us, length us, event | category | flops | bytes accessed | tf_op | source)
XLA Modules:
  0.0 47.1 jit_solution(5489752095351510535)
XLA Ops:
  0.0 45.0 %shard_map.154 = bf16[8,200,256]{2,1,0:T(8,128)(2,1)} custom-call(bf16[8,200,256]{2,1,0:T(8,128)(2,1)} %queries.1, bf16[200,256]{1,0:T(8,128)(2,1)} %query_pos.1, bf16[8,256,256]{2,1,0:T(8,128)(2,1)} %pixels.1, bf16[256,256]{1,0:T(8,128)(2,1)} %pixel_pos.1, s32[8,200,256]{2,1,0:T(8,128)} %masks.1, bf16[256,256]{1,0:T(8,128)(2,1)} %wq_cross.1, ...), custom_call_target="tpu_custom_call" | custom-call | tf_op jit(solution)/shard_map/pallas_call | solution.py:485
  45.0 2.1 %copy.18 = bf16[8,200,256]{2,1,0:T(8,128)(2,1)} copy(bf16[8,200,256]{2,1,0:T(8,128)(2,1)} %shard_map.154) | data formatting | bytes 1638400
where the time goes:
time: 47.3 us; the launch traced here: 47.1 us
  Pallas kernels  45 us (95%)
  local copies, waits for them, and re-layouts  2.09 us (4%)
    pallas_call x1, Pallas kernels, local(): pl.pallas_call(functools.partial(kernel, n), out_shape=jax.ShapeDtypeStru...  45 us
    unnamed x1, local copies, waits for them, and re-layouts  2.09 us

commit v1 on v0

--- a/solution.py
+++ b/solution.py
@@ -70,13 +70,17 @@
     win_v,
     wout_v,
     gf_v,
-    wqt,
-    wvt,
+    wkt,
     wvst,
+    key_v,
+    val_v,
+    cq_v,
     send_s,
     send_t,
+    send_f,
     recv_s,
     recv_t,
+    recv_f,
     att,
     gath,
     load_sem,
@@ -90,12 +94,15 @@
     xpos_r,
     ss_sem,
     st_sem,
+    sf_sem,
     rs_sem,
     rt_sem,
+    rf_sem,
     att_s,
     att_r,
     g1_s,
     g2_s,
+    g3_s,
     g_r,
     out_sem,
 ):
@@ -162,11 +169,9 @@
     pix_own.start()
     mask_own.start()
 
-    ident = eye(npix)
     for c in load[:6]:
         c.wait()
-    wqt[...] = nt(eye(width), wq_v[...]).astype(BF16)
-    wvt[...] = nt(eye(width), wv_v[...]).astype(BF16)
+    wkt[...] = nt(eye(width), wk_v[...]).astype(BF16)
 
     pl.semaphore_wait(barrier, n - 1)
     xpos = remote(pixel_pos, pos_v.at[1], xpos_s, xpos_r, mate)
@@ -182,74 +187,85 @@
             masks.at[base_other + j], mask_v.at[1, j], xmask_s.at[j], xmask_r.at[j], mate
         )
 
-    for j in range(half):
-        xmask(j).start()
-        xpix(j).start()
+    for jj in range(half):
+        xmask(lax.rem(jj + pair, half)).start()
+        xpix(lax.rem(jj + pair, half)).start()
     for c in load[6:]:
         c.start()
     pix_own.wait()
     mask_own.wait()
+
+    lane_head = lax.broadcasted_iota(jnp.int32, (nq, width), 1) // hd
+    lane = lax.broadcasted_iota(jnp.int32, (nq, 128), 1)
+
+    def project(side, j):
+        pix = pix_v[side, j]
+        key_in = (pix.astype(F32) + pos_v[side].astype(F32)).astype(BF16)
+        key_t = nt(wkt[...], key_in).astype(BF16)
+        value = nn(pix, wv_v[...]).astype(BF16)
+        return key_t, value
+
+    def own_side(j, carry):
+        qin = (q_mine[j].astype(F32) + qpos_v[...].astype(F32)).astype(BF16)
+        cq_v[j] = nn(qin, wq_v[...]).astype(BF16)
+        key_v[j], val_v[j] = project(0, j)
+        return carry
+
+    lax.fori_loop(0, half, own_side, 0)
     xpos.wait()
 
-    def send_s_copy(j, o):
+    def send_copies(j, o):
         owner = (base + j) * spread * 2 + o
-        return owner, remote(
-            send_s.at[j, o], recv_s.at[pair], ss_sem.at[j, o], rs_sem.at[pair], owner
-        )
-
-    def send_t_copy(j, o):
-        owner = (base + j) * spread * 2 + o
-        return owner, remote(
-            send_t.at[j, o], recv_t.at[pair], st_sem.at[j, o], rt_sem.at[pair], owner
-        )
-
-    def one_image(j, carry):
+        return owner, (
+            remote(send_f.at[j], recv_f.at[pair], sf_sem.at[j, o], rf_sem.at[pair], owner),
+            remote(send_t.at[j, o], recv_t.at[pair], st_sem.at[j, o], rt_sem.at[pair], owner),
+            remote(send_s.at[j, o], recv_s.at[pair], ss_sem.at[j, o], rs_sem.at[pair], owner),
+        )
+
+    def one_image(jj, carry):
+        j = lax.rem(jj + pair, half)
         xmask(j).wait()
         xpix(j).wait()
-        qin = (q_mine[j].astype(F32) + qpos_v[...].astype(F32)).astype(BF16)
-        cqt = nt(wqt[...], qin).astype(BF16)
-        keys, values, seen = [], [], []
-        for side in range(2):
-            pix = pix_v[side, j]
-            key_in = (pix.astype(F32) + pos_v[side].astype(F32)).astype(BF16)
-            keys.append(nn(key_in, wk_v[...]).astype(BF16))
-            values.append(nt(wvt[...], pix).astype(BF16))
-            seen.append(nt(ident, mask_v[side, j].astype(F32).astype(BF16)))
-        key = jnp.concatenate(keys, axis=0)
-        value = jnp.concatenate(values, axis=1)
-        seen = jnp.concatenate(seen, axis=0)
-        found = jnp.max(seen, axis=0, keepdims=True)
+        cq = cq_v[j].astype(F32)
+        key, value = project(1, j)
+        key = jnp.concatenate([key_v[j], key], axis=1)
+        value = jnp.concatenate([val_v[j], value], axis=0)
+        seen = jnp.concatenate([mask_v[0, j], mask_v[1, j]], axis=1).astype(F32)
+        found = jnp.max(seen, axis=1, keepdims=True)
         bias = jnp.where(jnp.logical_or(seen > 0.5, found < 0.5), 0.0, NEG)
+        stats = jnp.where(lane == 4 * hp, found, 0.0)
+        rows = jnp.zeros((nq, width), F32)
         for h in range(HEADS):
-            pieces = [cqt[h * hd : (h + 1) * hd]]
-            if h:
-                pieces.insert(0, jnp.zeros((h * hd, nq), BF16))
-            if h < HEADS - 1:
-                pieces.append(jnp.zeros((width - (h + 1) * hd, nq), BF16))
-            score = nn(key, jnp.concatenate(pieces, axis=0)) + bias
-            top = jnp.max(score, axis=0, keepdims=True)
+            query = jnp.where(lane_head == h, cq, 0.0).astype(BF16)
+            score = nn(query, key) + bias
+            top = jnp.max(score, axis=1, keepdims=True)
             weight = jnp.exp2((score - top) * scale)
-            total = jnp.sum(weight, axis=0, keepdims=True)
-            summed = nn(value[h * hd : (h + 1) * hd], weight.astype(BF16))
+            total = jnp.sum(weight, axis=1, keepdims=True)
+            rows = jnp.where(lane_head == h, nn(weight.astype(BF16), value), rows)
             o, r = h // hp, h % hp
-            send_s[j, o, r * hd : (r + 1) * hd, :] = summed.astype(BF16)
-            send_t[j, o, r : r + 1, :] = top
-            send_t[j, o, hp + r : hp + r + 1, :] = total
+            stats = jnp.where(lane == o * 2 * hp + r, top, stats)
+            stats = jnp.where(lane == o * 2 * hp + hp + r, total, stats)
+        rows = rows.astype(BF16)
+        stats = jnp.transpose(stats)
         for o in range(2):
-            send_t[j, o, 2 * hp : 2 * hp + 1, :] = found
+            send_t[j, o] = stats[o * 2 * hp : (o + 1) * 2 * hp]
+        send_f[j] = stats[4 * hp : 4 * hp + 1]
         for o in range(2):
-            owner, copy_s = send_s_copy(j, o)
-            _, copy_t = send_t_copy(j, o)
+            send_s[j, o] = rows[:, o * part : (o + 1) * part]
+        for o in range(2):
+            owner, copies = send_copies(j, o)
 
             @pl.when(owner != me)
             def _():
-                copy_t.start()
-                copy_s.start()
+                for copy in copies:
+                    copy.start()
 
             @pl.when(owner == me)
             def _():
-                pltpu.make_async_copy(send_t.at[j, o], recv_t.at[pair], rt_sem.at[pair]).start()
-                pltpu.make_async_copy(send_s.at[j, o], recv_s.at[pair], rs_sem.at[pair]).start()
+                here = pltpu.make_async_copy
+                here(send_f.at[j], recv_f.at[pair], rf_sem.at[pair]).start()
+                here(send_t.at[j, o], recv_t.at[pair], rt_sem.at[pair]).start()
+                here(send_s.at[j, o], recv_s.at[pair], rs_sem.at[pair]).start()
 
         return carry
 
@@ -259,15 +275,18 @@
         c.wait()
     wvst[...] = nt(eye(width), wqkv_v[:, 2 * width :]).astype(BF16)
 
+    ident_p = eye(part)
+
     def fold(k, carry):
         top, total, flag, acc = carry
         slot = lax.rem(pair + k, npairs)
+        pltpu.make_async_copy(recv_f.at[slot], recv_f.at[slot], rf_sem.at[slot]).wait()
         pltpu.make_async_copy(recv_t.at[slot], recv_t.at[slot], rt_sem.at[slot]).wait()
         pltpu.make_async_copy(recv_s.at[slot], recv_s.at[slot], rs_sem.at[slot]).wait()
         new_top = recv_t[slot, 0:hp, :]
         new_total = recv_t[slot, hp : 2 * hp, :]
-        new_flag = recv_t[slot, 2 * hp : 2 * hp + 1, :]
-        new = recv_s[slot].astype(F32)
+        new_flag = recv_f[slot]
+        new = nt(ident_p, recv_s[slot])
         best = jnp.maximum(flag, new_flag)
         a = jnp.where(flag == best, top, NEG)
         b = jnp.where(new_flag == best, new_top, NEG)
@@ -287,6 +306,11 @@
     def gather_copy(ssem, image, c, dev):
         ref = gath.at[image, c]
         return remote(ref, ref, ssem, g_r.at[image, c], dev)
+
+    relay = spread == 1 and npairs % 2 == 0
+    step = 2 if relay else 1
+    pair_across = pair + 1 - 2 * lax.rem(pair, 2)
+    across = pair_across * 2 + core
 
     def owner_work():
         start = (
@@ -313,7 +337,6 @@
         both = nn(self_in, wqkv_v[:, : 2 * width]).astype(BF16)
         sq, sk = both[:, :width], both[:, width:]
         svt = nt(wvst[...], after_cross).astype(BF16)
-        lane_head = lax.broadcasted_iota(jnp.int32, (nq, width), 1) // hd
         outs = []
         for h in range(HEADS):
             key = jnp.where(lane_head == h, sk.astype(F32), 0.0).astype(BF16)
@@ -331,12 +354,16 @@
         for c in range(2):
             gath[my_image, c] = result[:, c * part : (c + 1) * part]
 
+        if relay:
+            gather_copy(g3_s.at[my_image], my_image, core, across).start()
+
         def spread_out(k, carry):
+            k = k * step
             dev = lax.rem(pair + k, npairs) * 2 + core
             gather_copy(g1_s.at[k], my_image, core, dev).start()
             return carry
 
-        lax.fori_loop(1, npairs, spread_out, 0)
+        lax.fori_loop(1, npairs // step, spread_out, 0)
         swap.wait_send()
 
     is_owner = lax.rem(pair, spread) == 0
@@ -352,44 +379,82 @@
             out_sem.at[image, c],
         )
 
-    def arrive_near(k, carry):
-        image = lax.rem(my_image + k, images)
-        not_mine = jnp.logical_or(image != my_image, jnp.logical_not(is_owner))
-
-        @pl.when(not_mine)
-        def _():
-            ref = gath.at[image, core]
-            pltpu.make_async_copy(ref, ref, g_r.at[image, core]).wait()
+    def arrived(image, c):
+        ref = gath.at[image, c]
+        pltpu.make_async_copy(ref, ref, g_r.at[image, c]).wait()
+
+    def relayed():
+        for c in range(2):
+            write_out(my_image, c).start()
+
+        def direct(k, carry):
+            image = lax.rem(pair + 2 * k, images)
+            arrived(image, core)
+            gather_copy(g3_s.at[image], image, core, across).start()
             gather_copy(g2_s.at[image], image, core, mate).start()
-
-        write_out(image, core).start()
-        return carry
-
-    lax.fori_loop(0, images, arrive_near, 0)
-
-    def arrive_far(k, carry):
-        image = lax.rem(my_image + k, images)
-        not_mine = jnp.logical_or(image != my_image, jnp.logical_not(is_owner))
-
-        @pl.when(not_mine)
-        def _():
-            ref = gath.at[image, other]
-            pltpu.make_async_copy(ref, ref, g_r.at[image, other]).wait()
-
-        write_out(image, other).start()
-        return carry
-
-    lax.fori_loop(0, images, arrive_far, 0)
+            write_out(image, core).start()
+            return carry
+
+        def second(k, carry):
+            image = lax.rem(pair_across + 2 * k, images)
+            arrived(image, core)
+            gather_copy(g2_s.at[image], image, core, mate).start()
+            write_out(image, core).start()
+            return carry
+
+        def third(k, carry):
+            image = lax.rem(pair + k, images)
+            arrived(image, other)
+            write_out(image, other).start()
+            return carry
+
+        lax.fori_loop(1, images // 2, direct, 0)
+        lax.fori_loop(0, images // 2, second, 0)
+        lax.fori_loop(1, images, third, 0)
+
+    def plain():
+        def arrive_near(k, carry):
+            image = lax.rem(my_image + k, images)
+            not_mine = jnp.logical_or(image != my_image, jnp.logical_not(is_owner))
+
+            @pl.when(not_mine)
+            def _():
+                ref = gath.at[image, core]
+                pltpu.make_async_copy(ref, ref, g_r.at[image, core]).wait()
+                gather_copy(g2_s.at[image], image, core, mate).start()
+
+            write_out(image, core).start()
+            return carry
+
+        lax.fori_loop(0, images, arrive_near, 0)
+
+        def arrive_far(k, carry):
+            image = lax.rem(my_image + k, images)
+            not_mine = jnp.logical_or(image != my_image, jnp.logical_not(is_owner))
+
+            @pl.when(not_mine)
+            def _():
+                ref = gath.at[image, other]
+                pltpu.make_async_copy(ref, ref, g_r.at[image, other]).wait()
+
+            write_out(image, other).start()
+            return carry
+
+        lax.fori_loop(0, images, arrive_far, 0)
+
+    if relay:
+        relayed()
+    else:
+        plain()
 
     def drain_sends(j, carry):
         for o in range(2):
-            owner, copy_s = send_s_copy(j, o)
-            _, copy_t = send_t_copy(j, o)
+            owner, copies = send_copies(j, o)
 
             @pl.when(owner != me)
             def _():
-                copy_s.wait_send()
-                copy_t.wait_send()
+                for copy in copies:
+                    copy.wait_send()
 
         return carry
 
@@ -397,11 +462,20 @@
 
     def drain_spread():
         def body(k, carry):
+            k = k * step
             dev = lax.rem(pair + k, npairs) * 2 + core
             gather_copy(g1_s.at[k], my_image, core, dev).wait_send()
             return carry
 
-        lax.fori_loop(1, npairs, body, 0)
+        lax.fori_loop(1, npairs // step, body, 0)
+        if relay:
+
+            def across_body(k, carry):
+                image = lax.rem(pair + 2 * k, images)
+                gather_copy(g3_s.at[image], image, core, across).wait_send()
+                return carry
+
+            lax.fori_loop(0, images // 2, across_body, 0)
 
     if spread == 1:
         drain_spread()
@@ -455,11 +529,15 @@
         pltpu.VMEM((1, width), F32),
         pltpu.VMEM((width, width), BF16),
         pltpu.VMEM((width, width), BF16),
-        pltpu.VMEM((width, width), BF16),
-        pltpu.VMEM((half, 2, part, nq), BF16),
-        pltpu.VMEM((half, 2, 2 * hp + 1, nq), F32),
-        pltpu.VMEM((npairs, part, nq), BF16),
-        pltpu.VMEM((npairs, 2 * hp + 1, nq), F32),
+        pltpu.VMEM((half, width, npix), BF16),
+        pltpu.VMEM((half, npix, width), BF16),
+        pltpu.VMEM((half, nq, width), BF16),
+        pltpu.VMEM((half, 2, nq, part), BF16),
+        pltpu.VMEM((half, 2, 2 * hp, nq), F32),
+        pltpu.VMEM((half, 1, nq), F32),
+        pltpu.VMEM((npairs, nq, part), BF16),
+        pltpu.VMEM((npairs, 2 * hp, nq), F32),
+        pltpu.VMEM((npairs, 1, nq), F32),
         pltpu.VMEM((2, part, nq), BF16),
         pltpu.VMEM((images, 2, nq, part), BF16),
         dma((15,)),
@@ -473,11 +551,14 @@
         dma,
         dma((half, 2)),
         dma((half, 2)),
+        dma((half, 2)),
+        dma((npairs,)),
         dma((npairs,)),
         dma((npairs,)),
         dma,
         dma((2,)),
         dma((npairs,)),
+        dma((images,)),
         dma((images,)),
         dma((images, 2)),
         dma((images, 2)),

time: 47.3 us -> 42.4 us (0.90)
  the two profiles are of different devices: /device:TPU:21 before, /device:TPU:1 now
where the time goes in v1:
time: 42.4 us; the launch traced here: 42.3 us
  Pallas kernels  40.2 us (95%)
  local copies, waits for them, and re-layouts  2.09 us (5%)
    pallas_call x1, Pallas kernels, local(): pl.pallas_call(functools.partial(kernel, n), out_shape=jax.ShapeDtypeStru...  40.2 us
    unnamed x1, local copies, waits for them, and re-layouts  2.09 us

profile of v1, /device:TPU:1, one launch (start us, length us, event | category | flops | bytes accessed | tf_op | source)
XLA Modules:
  0.0 42.3 jit_solution(8064947852955616218)
XLA Ops:
  0.0 40.2 %shard_map.154 = bf16[8,200,256]{2,1,0:T(8,128)(2,1)} custom-call(bf16[8,200,256]{2,1,0:T(8,128)(2,1)} %queries.1, bf16[200,256]{1,0:T(8,128)(2,1)} %query_pos.1, bf16[8,256,256]{2,1,0:T(8,128)(2,1)} %pixels.1, bf16[256,256]{1,0:T(8,128)(2,1)} %pixel_pos.1, s32[8,200,256]{2,1,0:T(8,128)} %masks.1, bf16[256,256]{1,0:T(8,128)(2,1)} %wq_cross.1, ...), custom_call_target="tpu_custom_call" | custom-call | tf_op jit(solution)/shard_map/pallas_call | solution.py:566
  40.2 2.1 %copy.18 = bf16[8,200,256]{2,1,0:T(8,128)(2,1)} copy(bf16[8,200,256]{2,1,0:T(8,128)(2,1)} %shard_map.154) | data formatting | bytes 1638400
